TPU v7x, 32 devices: a whole 2x2x4 slice. The times are simulated.
32 devices in a mesh: pipe: 2 (over core), dp: 8 (over z, y), mp: 2 (over x).
Axes of the slice: x: 2, y: 2, z: 4, core: 2. Of those that a mesh axis runs over, the one named last changes fastest.
Arguments:
- token_ids: int32 [2, 4096], P('pipe', 'dp'), may hold values from 0 to 32127, as said below
- embedded: bfloat16 [2, 4096, 4096], P('pipe', 'dp', 'mp'), may hold values from -720 to 720
- norm_gain: float32 [2, 4096], P('pipe', 'mp'), may hold values from 0.25 to 1.75
- proj_grad: bfloat16 [2, 4096, 2048], P('pipe', 'dp'), may hold values from -6 to 6
- proj_weight: bfloat16 [2, 4096, 2048], P('pipe', 'mp'), may hold values from -0.125 to 0.125
- stream_grad: bfloat16 [2, 4096, 4096], P('pipe', 'dp', 'mp'), may hold values from -6 to 6
Outputs:
- table_grad: float32 [32128, 2, 2048], P('dp', 'mp', 'pipe')
Inputs may be any that keep to these rules, and one draw needn't show every extreme that they name: `token_ids`: call block o the ids o * 4016 to (o + 1) * 4016 - 1. The 512 tokens of one stack on one index of dp hold at most 128 ids of any one block, and some block gets exactly 128 of them.
All inputs are finite; a program needn't handle non-finite values.
Results may differ from a plain program's by a relative error of at most 0.0029.
Values may be sent and summed in bfloat16 or wider, within the bound.
A program may use at most 128 MiB of HBM per device.

v0:
```python
import jax
import jax.numpy as jnp
from jax import lax
from jax.sharding import PartitionSpec as P

D = 4096
VOCAB = 32128
epsilon = 1e-06


def accumulate(got_rows, got_index, block_rows):
    width = got_rows.shape[-1]
    flat_rows = got_rows.reshape(-1, width)
    flat_index = got_index.reshape(-1)
    selector = (flat_index[None, :] == jnp.arange(block_rows, dtype=jnp.int32)[:, None]).astype(
        jnp.bfloat16
    )
    return jnp.dot(selector, flat_rows, preferred_element_type=jnp.float32)


def on_device(token_ids, embedded, norm_gain, proj_grad, proj_weight, stream_grad):
    projected = lax.dot_general(
        proj_grad[0], proj_weight[0], (((1,), (1,)), ((), ())), preferred_element_type=jnp.float32
    )
    inputs = embedded[0].astype(jnp.float32)
    scaled = projected * norm_gain[0][None, :]
    square_sum, mixed_sum = lax.psum(
        (jnp.sum(inputs * inputs, axis=1), jnp.sum(inputs * scaled, axis=1)), "mp"
    )
    inverse = lax.rsqrt(square_sum / D + epsilon)
    norm_back = (
        inverse[:, None] * scaled - inputs * (inverse * inverse * inverse * mixed_sum / D)[:, None]
    )
    grad_rows = (stream_grad[0].astype(jnp.float32) + norm_back).astype(jnp.bfloat16)
    replicas = lax.axis_size("dp")
    tokens_here = grad_rows.shape[0]
    capacity = max(2, 2 * tokens_here // replicas)
    block_rows = VOCAB // replicas
    token_row = token_ids[0]
    owners = token_row // block_rows
    local_row = token_row % block_rows
    matches = (owners[:, None] == jnp.arange(replicas, dtype=jnp.int32)[None, :]).astype(jnp.int32)
    earlier = jnp.cumsum(matches, axis=0) - matches
    position = owners * capacity + jnp.sum(earlier * matches, axis=1)
    placer = (
        position[None, :] == jnp.arange(replicas * capacity, dtype=jnp.int32)[:, None]
    ).astype(jnp.bfloat16)
    send_rows = jnp.dot(placer, grad_rows, preferred_element_type=jnp.float32).astype(jnp.bfloat16)
    send_rows = send_rows.reshape(replicas, capacity, grad_rows.shape[1])
    send_index = jnp.full((replicas * capacity,), block_rows, jnp.int32).at[position].set(local_row)
    send_index = send_index.reshape(replicas, capacity)
    paired_index = jnp.stack([send_index, send_index], axis=2)
    mixed_rows, mixed_index = (
        lax.all_to_all(send_rows, "pipe", split_axis=2, concat_axis=1, tiled=True),
        lax.all_to_all(paired_index, "pipe", split_axis=2, concat_axis=1, tiled=True),
    )
    got_rows, got_index = (
        lax.all_to_all(mixed_rows, "dp", split_axis=0, concat_axis=0, tiled=True),
        lax.all_to_all(mixed_index, "dp", split_axis=0, concat_axis=0, tiled=True),
    )
    half_table = accumulate(got_rows, got_index, block_rows)
    return half_table.reshape(block_rows, 1, half_table.shape[1])


def solution(mesh):
    return jax.shard_map(
        on_device,
        mesh=mesh,
        in_specs=(
            P("pipe", "dp"),
            P("pipe", "dp", "mp"),
            P("pipe", "mp"),
            P("pipe", "dp", None),
            P("pipe", "mp", None),
            P("pipe", "dp", "mp"),
        ),
        out_specs=P("dp", "mp", "pipe"),
        check_vma=False,
    )
```

profile of v0, /device:TPU:0, one launch (start us, length us, event | category | flops | bytes accessed | tf_op | source)
XLA Modules:
  0.0 245.0 jit_solution(3031371806581677621)
XLA Ops:
  0.0 0.9 compare_reduce_fusion
  0.9 0.7 broadcast_remainder_fusion
  1.6 1.1 reduce-window.6
  2.7 0.2 slice_reduce_fusion
  3.0 0.1 fusion.19
  3.1 0.7 compare_select_fusion
  3.8 2.4 scatter_custom_fusion
  6.3 0.6 pad_add_fusion
  6.8 3.2 %all-to-all-start = ((s32[8,128,2]{1,0,2:T(8,128)}), s32[8,128,2]{1,0,2:T(8,128)S(1)}, u32[]{:S(2)}, u32[]{:S(2)}) async-start(s32[8,128,2]{1,0,2:T(8,128)} %pad_add_fusion), calls=%async_computation | async-start | bytes 16384 | tf_op jit(solution)/shard_map/all_to_all | solution.py:55
  10.1 0.7 fusion.22
  10.8 0.0 copy-start.2
  10.8 10.0 %fusion.5 = (f32[512]{0:T(512)S(1)}, f32[512]{0:T(512)S(1)}, f32[512,2048]{1,0:T(8,128)}) fusion(bf16[1,512,2048]{2,1,0:T(8,128)(2,1)} %param.7, f32[2048]{0:T(1024)} %bitcast.84, bf16[1,2048,2048]{2,1,0:T(8,128)(2,1)} %param.10, bf16[1,512,2048]{2,1,0:T(8,128)(2,1)S(1)} %copy-done), kind=kOutput, calls=%fused_computation.10 | convolution fusion | flops 4301257728 | bytes 16789504 | tf_op jit(solution)/shard_map/dot_general | solution.py:22
  20.8 5.8 %all-reduce = (f32[512]{0:T(512)S(1)}, f32[512]{0:T(512)S(1)}) all-reduce(f32[512]{0:T(512)S(1)} %get-tuple-element.6, f32[512]{0:T(512)S(1)} %get-tuple-element.5), channel_id=1, replica_groups=mesh['pipe'=2,'dp'=8,'mp'=2] {'mp'}, use_global_device_ids=true, to_apply=%region_7.8 | all-reduce | flops 1024 | bytes 8192 | tf_op jit(solution)/shard_map/psum | solution.py:27
  26.7 8.1 %convolution_convert_fusion = bf16[1024,2048]{1,0:T(8,128)(2,1)} fusion(f32[512,2048]{1,0:T(8,128)} %get-tuple-element.17, bf16[1,512,2048]{2,1,0:T(8,128)(2,1)} %param.11, bf16[1,512,2048]{2,1,0:T(8,128)(2,1)} %param.7, f32[512]{0:T(512)S(1)} %get-tuple-element.16, f32[2048]{0:T(1024)S(1)} %bitcast.85, f32[512]{0:T(512)S(1)} %get-tuple-element.15, ...), kind=kOutput, calls=%fused_computation.15 | convolution fusion | flops 2158493696 | bytes 12597248 | tf_op jit(solution)/shard_map/dot_general | solution.py:48
  34.8 6.8 %copy.13 = bf16[8,128,2048]{1,0,2:T(8,128)(2,1)} copy(bf16[8,128,2048]{2,1,0:T(8,128)(2,1)} %bitcast.72) | data formatting | bytes 8388608 | tf_op jit(solution)/shard_map/reshape | solution.py:49
  41.6 5.6 %all-to-all-start.2 = ((bf16[8,128,2048]{1,0,2:T(8,128)(2,1)}), bf16[8,128,2048]{1,0,2:T(8,128)(2,1)}, u32[]{:S(2)}, u32[]{:S(2)}) async-start(bf16[8,128,2048]{1,0,2:T(8,128)(2,1)} %copy.13), calls=%async_computation.2 | async-start | bytes 8388608 | tf_op jit(solution)/shard_map/all_to_all | solution.py:54
  47.2 0.6 copy.12
  47.8 3.9 %all-to-all-done.2 = bf16[8,128,2048]{1,0,2:T(8,128)(2,1)} async-done(((bf16[8,128,2048]{1,0,2:T(8,128)(2,1)}), bf16[8,128,2048]{1,0,2:T(8,128)(2,1)}, u32[]{:S(2)}, u32[]{:S(2)}) %all-to-all-start.2) | async-done | bytes 4194336 | tf_op jit(solution)/shard_map/all_to_all | solution.py:54
  51.7 6.4 %all-to-all-start.1 = ((s32[8,256,1]{1,2,0:T(1,128)}), s32[8,256,1]{1,2,0:T(1,128)S(1)}, u32[]{:S(2)}, u32[]{:S(2)}) async-start(s32[8,256,1]{1,2,0:T(1,128)} %copy.12), calls=%async_computation.1 | async-start | bytes 16384 | tf_op jit(solution)/shard_map/all_to_all | solution.py:59
  58.0 6.6 %copy.15 = bf16[8,2,128,1024]{3,2,1,0:T(8,128)(2,1)} copy(bf16[8,2,128,1024]{2,0,3,1:T(8,128)(2,1)} %bitcast.25) | data formatting | bytes 8388608 | tf_op jit(solution)/shard_map/all_to_all | solution.py:54
  64.6 99.1 %all_to_all.46 = bf16[8,256,1024]{2,1,0:T(8,128)(2,1)S(1)} all-to-all(bf16[8,256,1024]{2,1,0:T(8,128)(2,1)} %bitcast.71), channel_id=1, replica_groups=mesh['pipe'=2,'dp'=8,'mp'=2] {'dp'}, dimensions={0} | all-to-all | bytes 8388608 | tf_op jit(solution)/shard_map/all_to_all | solution.py:58
  163.8 17.4 %fusion.2 = f32[4016,1,1024]{2,0,1:T(8,128)S(1)} fusion(bf16[2048,1024]{1,0:T(8,128)(2,1)S(1)} %bitcast.73, s32[2048]{0:T(1024)S(1)} %bitcast.81), kind=kOutput, calls=%fused_computation.4 | convolution fusion | flops 16852549632 | bytes 20652032 | tf_op jit(solution)/shard_map/dot_general | solution.py:18
  181.1 0.0 copy-start.1
  181.2 63.9 %copy.16 = f32[4016,1,1024]{2,1,0:T(1,128)} copy(f32[4016,1,1024]{2,0,1:T(8,128)S(1)} %fusion.2) | data formatting | bytes 32899072 | tf_op jit(solution)/shard_map/reshape | solution.py:62
  (12 shorter events, 0.1 us)
Async XLA Ops:
  0.0 10.8 %copy-start = (bf16[1,512,2048]{2,1,0:T(8,128)(2,1)S(1)}, bf16[1,512,2048]{2,1,0:T(8,128)(2,1)}, u32[]{:S(2)}) copy-start(bf16[1,512,2048]{2,1,0:T(8,128)(2,1)} %param.9) | copy-start | bytes 6291460
  6.8 34.7 %all-to-all-start = ((s32[8,128,2]{1,0,2:T(8,128)}), s32[8,128,2]{1,0,2:T(8,128)S(1)}, u32[]{:S(2)}, u32[]{:S(2)}) async-start(s32[8,128,2]{1,0,2:T(8,128)} %pad_add_fusion), calls=%async_computation | async-start | bytes 16384 | tf_op jit(solution)/shard_map/all_to_all | solution.py:55
  10.8 15.9 %copy-start.2 = (f32[1,2048]{1,0:T(1,128)S(1)}, f32[1,2048]{1,0:T(1,128)}, u32[]{:S(2)}) copy-start(f32[1,2048]{1,0:T(1,128)} %param.8) | copy-start | bytes 24580
  41.6 10.1 %all-to-all-start.2 = ((bf16[8,128,2048]{1,0,2:T(8,128)(2,1)}), bf16[8,128,2048]{1,0,2:T(8,128)(2,1)}, u32[]{:S(2)}, u32[]{:S(2)}) async-start(bf16[8,128,2048]{1,0,2:T(8,128)(2,1)} %copy.13), calls=%async_computation.2 | async-start | bytes 8388608 | tf_op jit(solution)/shard_map/all_to_all | solution.py:54
  51.7 13.0 %all-to-all-start.1 = ((s32[8,256,1]{1,2,0:T(1,128)}), s32[8,256,1]{1,2,0:T(1,128)S(1)}, u32[]{:S(2)}, u32[]{:S(2)}) async-start(s32[8,256,1]{1,2,0:T(1,128)} %copy.12), calls=%async_computation.1 | async-start | bytes 16384 | tf_op jit(solution)/shard_map/all_to_all | solution.py:59
  181.1 63.9 %copy-start.1 = (bf16[1,512,2048]{2,1,0:T(8,128)(2,1)S(1)}, bf16[1,512,2048]{2,1,0:T(8,128)(2,1)}, u32[]{:S(2)}) copy-start(bf16[1,512,2048]{2,1,0:T(8,128)(2,1)} %param.9) | copy-start | bytes 6291460
where the time goes:
time: 246 us; the launch traced here: 245 us
  blocking collectives  105 us (43%)
  local copies, waits for them, and re-layouts  80.5 us (33%)
  matrix products  35.5 us (14%)
  starting transfers between devices  15.2 us (6%)
  other arithmetic  4.86 us (2%)
  waiting for transfers between devices  3.88 us (2%)
    all_to_all x1, blocking collectives, on_device(): lax.all_to_all(mixed_rows, 'dp', split_axis=0, concat_axis=0, tiled=True)  99.1 us
    reshape x1, local copies, waits for them, and re-layouts, on_device(): return half_table.reshape(block_rows, 1, half_table.shape[1])  63.9 us
    dot_general x1, matrix products, accumulate(): return jnp.dot(selector, flat_rows, preferred_element_type=jnp.float32)  17.4 us
    dot_general x1, matrix products, on_device(): lax.dot_general(proj_grad[0], proj_weight[0], (((1,), (1,)), ((), ())), p...  10 us
    dot_general x1, matrix products, on_device(): jnp.dot(placer, grad_rows, preferred_element_type=jnp.float32)  8.1 us
    reshape x1, local copies, waits for them, and re-layouts, on_device(): send_rows = send_rows.reshape(replicas, capacity, grad_rows.shape[1])  6.76 us
    all_to_all x1, local copies, waits for them, and re-layouts, on_device(): lax.all_to_all(send_rows, 'pipe', split_axis=2, concat_axis=1, tiled=True)  6.6 us
    all_to_all x1, starting transfers between devices, on_device(): lax.all_to_all(mixed_index, 'dp', split_axis=0, concat_axis=0, tiled=True)  6.37 us
  transfers between devices with their start and end apart: 3, of which 1 were waited for; matrix products, arithmetic and copies ran while one was open for 13% of the time, Pallas kernels for 0%

commit v1 on v0

--- a/solution.py
+++ b/solution.py
@@ -51,7 +51,12 @@
     send_index = send_index.reshape(replicas, capacity)
     paired_index = jnp.stack([send_index, send_index], axis=2)
     mixed_rows, mixed_index = (
-        lax.all_to_all(send_rows, "pipe", split_axis=2, concat_axis=1, tiled=True),
+        jnp.concatenate(
+            lax.all_to_all(
+                jnp.stack(jnp.split(send_rows, lax.axis_size("pipe"), 2), 0), "pipe", 0, 0
+            ),
+            1,
+        ),
         lax.all_to_all(paired_index, "pipe", split_axis=2, concat_axis=1, tiled=True),
     )
     got_rows, got_index = (

time: 246 us -> 238 us (0.967)
  local copies, waits for them, and re-layouts: 80.5 us -> 72.4 us
    reshape x1 -> x0, local copies, waits for them, and re-layouts: 6.76 us -> none  [on_device(): send_rows = send_rows.reshape(replicas, capacity, grad_rows.shape[1])]
  transfers between devices with their start and end apart: 3 -> 3, of which waited for: 1 -> 2; matrix products, arithmetic and copies ran while one was open for 13% -> 11% of each run, Pallas kernels for 0% -> 0%
where the time goes in v1:
time: 238 us; the launch traced here: 237 us
  blocking collectives  103 us (43%)
  local copies, waits for them, and re-layouts  72.4 us (30%)
  matrix products  33.6 us (14%)
  starting transfers between devices  15.2 us (6%)
  other arithmetic  7.23 us (3%)
  waiting for transfers between devices  5.59 us (2%)
    all_to_all x1, blocking collectives, on_device(): lax.all_to_all(mixed_rows, 'dp', split_axis=0, concat_axis=0, tiled=True)  97.4 us
    reshape x1, local copies, waits for them, and re-layouts, on_device(): return half_table.reshape(block_rows, 1, half_table.shape[1])  63.9 us
    dot_general x1, matrix products, accumulate(): return jnp.dot(selector, flat_rows, preferred_element_type=jnp.float32)  17.4 us
    dot_general x1, matrix products, on_device(): lax.dot_general(proj_grad[0], proj_weight[0], (((1,), (1,)), ((), ())), p...  10 us
    all_to_all x1, starting transfers between devices, on_device(): lax.all_to_all(mixed_index, 'dp', split_axis=0, concat_axis=0, tiled=True)  6.38 us
    dot_general x1, matrix products, on_device(): jnp.dot(placer, grad_rows, preferred_element_type=jnp.float32)  6.18 us
    psum x1, blocking collectives, on_device(): lax.psum((jnp.sum(inputs * inputs, axis=1), jnp.sum(inputs * scaled, axis...  5.84 us
    all_to_all x1, starting transfers between devices, on_device(): lax.all_to_all(jnp.stack(jnp.split(send_rows, lax.axis_size('pipe'), 2),...  5.62 us
  transfers between devices with their start and end apart: 3, of which 2 were waited for; matrix products, arithmetic and copies ran while one was open for 11% of the time, Pallas kernels for 0%

profile of v1, /device:TPU:0, one launch (start us, length us, event | category | flops | bytes accessed | tf_op | source)
XLA Modules:
  0.0 237.4 jit_solution(5326881770113705145)
XLA Ops:
  0.0 0.9 compare_reduce_fusion
  0.9 0.7 broadcast_remainder_fusion
  1.6 1.1 reduce-window.6
  2.7 0.2 slice_reduce_fusion
  3.0 0.1 fusion.19
  3.1 0.7 compare_select_fusion
  3.8 2.4 %scatter_custom_fusion = s32[1024]{0:T(1024)S(1)} fusion(s32[512]{0:T(512)S(1)} %bitcast.86, s32[512]{0:T(512)S(1)} %get-tuple-element.13, s32[]{:T(128)} %constant.30.clone.1), kind=kCustom, calls=%fused_computation.51 | custom fusion | bytes 4100 | tf_op jit(solution)/shard_map/scatter | solution.py:50
  6.3 0.6 pad_add_fusion
  6.8 3.2 %all-to-all-start = ((s32[8,128,2]{1,0,2:T(8,128)}), s32[8,128,2]{1,0,2:T(8,128)S(1)}, u32[]{:S(2)}, u32[]{:S(2)}) async-start(s32[8,128,2]{1,0,2:T(8,128)} %pad_add_fusion), calls=%async_computation | async-start | bytes 16384 | tf_op jit(solution)/shard_map/all_to_all | solution.py:60
  10.1 0.7 fusion.22
  10.8 10.0 %fusion.5 = (f32[512]{0:T(512)S(1)}, f32[512]{0:T(512)S(1)}, f32[512,2048]{1,0:T(8,128)}) fusion(bf16[1,512,2048]{2,1,0:T(8,128)(2,1)} %param.7, f32[2048]{0:T(1024)} %bitcast.87, bf16[1,2048,2048]{2,1,0:T(8,128)(2,1)} %param.10, bf16[1,512,2048]{2,1,0:T(8,128)(2,1)S(1)} %copy-done), kind=kOutput, calls=%fused_computation.10 | convolution fusion | flops 4301257728 | bytes 16789504 | tf_op jit(solution)/shard_map/dot_general | solution.py:22
  20.8 5.8 %all-reduce = (f32[512]{0:T(512)S(1)}, f32[512]{0:T(512)S(1)}) all-reduce(f32[512]{0:T(512)S(1)} %get-tuple-element.6, f32[512]{0:T(512)S(1)} %get-tuple-element.5), channel_id=1, replica_groups=mesh['pipe'=2,'dp'=8,'mp'=2] {'mp'}, use_global_device_ids=true, to_apply=%region_7.8 | all-reduce | flops 1024 | bytes 8192 | tf_op jit(solution)/shard_map/psum | solution.py:27
  26.7 6.2 %convolution_convert_fusion = bf16[1024,2048]{1,0:T(8,128)(2,1)S(1)} fusion(f32[512,2048]{1,0:T(8,128)} %get-tuple-element.19, bf16[1,512,2048]{2,1,0:T(8,128)(2,1)} %param.11, bf16[1,512,2048]{2,1,0:T(8,128)(2,1)} %param.7, f32[512]{0:T(512)S(1)} %get-tuple-element.18, f32[2048]{0:T(1024)S(1)} %bitcast.88, f32[512]{0:T(512)S(1)} %get-tuple-element.17, ...), kind=kOutput, calls=%fused_computation.16 | convolution fusion | flops 2158493696 | bytes 12597248 | tf_op jit(solution)/shard_map/dot_general | solution.py:48
  32.9 0.4 slice_bitcast_fusion.1
  33.3 2.4 %pad_maximum_fusion = bf16[2,8,128,1024]{3,2,1,0:T(8,128)(2,1)} fusion(bf16[1,8,128,1024]{3,2,1,0:T(8,128)(2,1)S(1)} %get-tuple-element.12, bf16[1,8,128,1024]{3,2,1,0:T(8,128)(2,1)S(1)} %get-tuple-element.11), kind=kLoop, calls=%fused_computation.15 | loop fusion | flops 2097152 | bytes 8388608 | tf_op jit(solution)/shard_map/stack | solution.py:56
  35.7 5.6 %all-to-all-start.2 = ((bf16[2,8,128,1024]{3,2,1,0:T(8,128)(2,1)}), bf16[2,8,128,1024]{3,2,1,0:T(8,128)(2,1)}, u32[]{:S(2)}, u32[]{:S(2)}) async-start(bf16[2,8,128,1024]{3,2,1,0:T(8,128)(2,1)} %pad_maximum_fusion), calls=%async_computation.2 | async-start | bytes 8388608 | tf_op jit(solution)/shard_map/all_to_all | solution.py:55
  41.3 0.6 copy.10
  41.9 3.9 %all-to-all-done.2 = bf16[2,8,128,1024]{3,2,1,0:T(8,128)(2,1)} async-done(((bf16[2,8,128,1024]{3,2,1,0:T(8,128)(2,1)}), bf16[2,8,128,1024]{3,2,1,0:T(8,128)(2,1)}, u32[]{:S(2)}, u32[]{:S(2)}) %all-to-all-start.2) | async-done | bytes 4194336 | tf_op jit(solution)/shard_map/all_to_all | solution.py:55
  45.8 6.4 %all-to-all-start.1 = ((s32[8,256,1]{1,2,0:T(1,128)}), s32[8,256,1]{1,2,0:T(1,128)S(1)}, u32[]{:S(2)}, u32[]{:S(2)}) async-start(s32[8,256,1]{1,2,0:T(1,128)} %copy.10), calls=%async_computation.1 | async-start | bytes 16384 | tf_op jit(solution)/shard_map/all_to_all | solution.py:64
  52.2 4.8 %copy.11 = bf16[2,8,128,1024]{3,2,0,1:T(8,128)(2,1)} copy(bf16[2,8,128,1024]{3,2,1,0:T(8,128)(2,1)} %all-to-all-done.2) | data formatting | bytes 8388608 | tf_op jit(solution)/shard_map/all_to_all | solution.py:55
  57.0 1.7 all-to-all-done.1
  58.7 97.4 %all_to_all.33 = bf16[8,256,1024]{2,1,0:T(8,128)(2,1)S(1)} all-to-all(bf16[8,256,1024]{2,1,0:T(8,128)(2,1)} %bitcast.74), channel_id=1, replica_groups=mesh['pipe'=2,'dp'=8,'mp'=2] {'dp'}, dimensions={0} | all-to-all | bytes 8388608 | tf_op jit(solution)/shard_map/all_to_all | solution.py:63
  156.1 17.4 %fusion.2 = f32[4016,1,1024]{2,0,1:T(8,128)S(1)} fusion(bf16[2048,1024]{1,0:T(8,128)(2,1)S(1)} %bitcast.76, s32[2048]{0:T(1024)S(1)} %bitcast.84), kind=kOutput, calls=%fused_computation.4 | convolution fusion | flops 16852549632 | bytes 20652032 | tf_op jit(solution)/shard_map/dot_general | solution.py:18
  173.5 63.9 %copy.12 = f32[4016,1,1024]{2,1,0:T(1,128)} copy(f32[4016,1,1024]{2,0,1:T(8,128)S(1)} %fusion.2) | data formatting | bytes 32899072 | tf_op jit(solution)/shard_map/reshape | solution.py:67
  (13 shorter events, 0.1 us)
Async XLA Ops:
  0.0 10.8 %copy-start = (bf16[1,512,2048]{2,1,0:T(8,128)(2,1)S(1)}, bf16[1,512,2048]{2,1,0:T(8,128)(2,1)}, u32[]{:S(2)}) copy-start(bf16[1,512,2048]{2,1,0:T(8,128)(2,1)} %param.9) | copy-start | bytes 6291460
  6.8 28.8 %all-to-all-start = ((s32[8,128,2]{1,0,2:T(8,128)}), s32[8,128,2]{1,0,2:T(8,128)S(1)}, u32[]{:S(2)}, u32[]{:S(2)}) async-start(s32[8,128,2]{1,0,2:T(8,128)} %pad_add_fusion), calls=%async_computation | async-start | bytes 16384 | tf_op jit(solution)/shard_map/all_to_all | solution.py:60
  10.8 15.9 %copy-start.2 = (f32[1,2048]{1,0:T(1,128)S(1)}, f32[1,2048]{1,0:T(1,128)}, u32[]{:S(2)}) copy-start(f32[1,2048]{1,0:T(1,128)} %param.8) | copy-start | bytes 24580
  35.7 10.1 %all-to-all-start.2 = ((bf16[2,8,128,1024]{3,2,1,0:T(8,128)(2,1)}), bf16[2,8,128,1024]{3,2,1,0:T(8,128)(2,1)}, u32[]{:S(2)}, u32[]{:S(2)}) async-start(bf16[2,8,128,1024]{3,2,1,0:T(8,128)(2,1)} %pad_maximum_fusion), calls=%async_computation.2 | async-start | bytes 8388608 | tf_op jit(solution)/shard_map/all_to_all | solution.py:55
  45.8 12.9 %all-to-all-start.1 = ((s32[8,256,1]{1,2,0:T(1,128)}), s32[8,256,1]{1,2,0:T(1,128)S(1)}, u32[]{:S(2)}, u32[]{:S(2)}) async-start(s32[8,256,1]{1,2,0:T(1,128)} %copy.10), calls=%async_computation.1 | async-start | bytes 16384 | tf_op jit(solution)/shard_map/all_to_all | solution.py:64
  173.5 63.9 %copy-start.1 = (bf16[1,512,2048]{2,1,0:T(8,128)(2,1)S(1)}, bf16[1,512,2048]{2,1,0:T(8,128)(2,1)}, u32[]{:S(2)}) copy-start(bf16[1,512,2048]{2,1,0:T(8,128)(2,1)} %param.9) | copy-start | bytes 6291460
